TPU v7x, 32 devices: a whole 2x2x4 slice. The times are simulated.
32 devices in a mesh: dp: 4 (over z), tp: 8 (over y, x, core).
Axes of the slice: x: 2, y: 2, z: 4, core: 2. Of those that a mesh axis runs over, the one named last changes fastest.
Arguments:
- x: bfloat16 [8, 1024, 4096], P('dp'), parts along dimension 0
- positions: int32 [8, 1024], P('dp'), parts along dimension 0
- lengths: int32 [8], P('dp'), parts along dimension 0
- w_q: bfloat16 [2, 4096, 4096], P(None, None, 'tp')
- w_k: bfloat16 [2, 4096, 1024], P(None, None, 'tp')
- w_v: bfloat16 [2, 4096, 1024], P(None, None, 'tp')
- w_o: bfloat16 [2, 4096, 4096], P(None, 'tp')
- w_gate: bfloat16 [2, 4096, 14336], P(None, None, 'tp')
- w_up: bfloat16 [2, 4096, 14336], P(None, None, 'tp')
- w_down: bfloat16 [2, 14336, 4096], P(None, 'tp')
- norm_gain: float32 [2, 4096], replicated
- q_gain: float32 [2, 32, 128], P(None, 'tp')
- k_gain: float32 [2, 8, 128], P(None, 'tp')
Outputs:
- output 1: bfloat16 [8, 1024, 4096], P('dp'), parts along dimension 0
- output 2: bfloat16 [2, 8, 1024, 8, 128], P(None, 'dp', None, 'tp'), parts along dimension 1
- output 3: bfloat16 [2, 8, 1024, 8, 128], P(None, 'dp', None, 'tp'), parts along dimension 1
There are 4 independent parts. A program takes and returns all parts, laid end to end along the dimension named above; an argument that names none is the same for every part.
All inputs are finite; a program needn't handle non-finite values.
Results may differ from a plain program's by a relative error of at most 0.0162269.
Values are sent between devices in bfloat16 or wider.
A program may use at most 1 GiB of HBM per device.

v0:
```python
import jax
import jax.numpy as jnp
from jax import lax
from jax.sharding import PartitionSpec as P

HEAD_DIM = 128
ROPE_THETA = 75000000.0
NORM_EPS = 1e-5


def norm_rows(values, gain_vec):
    as_float = values.astype(jnp.float32)
    row_mean = jnp.mean(as_float, axis=-1, keepdims=True)
    centered = as_float - row_mean
    variance = jnp.mean(centered * centered, axis=-1, keepdims=True)
    return centered * lax.rsqrt(variance + NORM_EPS) * gain_vec


def rope_tables(positions):
    exponents = jnp.arange(HEAD_DIM // 2, dtype=jnp.float32) * (2.0 / HEAD_DIM)
    angles = positions.astype(jnp.float32)[:, :, None] * ROPE_THETA ** (-exponents)
    return jnp.cos(angles)[:, :, None, :], jnp.sin(angles)[:, :, None, :]


def apply_rope(values, cos_table, sin_table):
    pairs = values.reshape(values.shape[:-1] + (HEAD_DIM // 2, 2))
    even_part = pairs[..., 0]
    odd_part = pairs[..., 1]
    rotated = jnp.stack([even_part * cos_table - odd_part * sin_table, odd_part * cos_table + even_part * sin_table], axis=-1)
    return rotated.reshape(values.shape)


def project(hidden, cos_table, sin_table, w_q, w_k, w_v, norm_gain, q_gain, k_gain):
    n_batch, n_rows = hidden.shape[0], hidden.shape[1]
    q_count = q_gain.shape[0]
    kv_count = k_gain.shape[0]
    normed = norm_rows(hidden, norm_gain).astype(jnp.bfloat16)
    q_proj = jnp.dot(normed, w_q, preferred_element_type=jnp.float32).reshape(n_batch, n_rows, q_count, HEAD_DIM)
    k_proj = jnp.dot(normed, w_k, preferred_element_type=jnp.float32).reshape(n_batch, n_rows, kv_count, HEAD_DIM)
    v_proj = jnp.dot(normed, w_v, preferred_element_type=jnp.float32).astype(jnp.bfloat16).reshape(n_batch, n_rows, kv_count, HEAD_DIM)
    q_rot = apply_rope(norm_rows(q_proj, q_gain), cos_table, sin_table).astype(jnp.bfloat16)
    k_rot = apply_rope(norm_rows(k_proj, k_gain), cos_table, sin_table).astype(jnp.bfloat16)
    q_grouped = q_rot.reshape(n_batch, n_rows, kv_count, q_count // kv_count, HEAD_DIM)
    return normed, q_grouped, k_rot, v_proj


def attend(q_grouped, k_rot, v_proj, lengths, row_start):
    n_batch, q_rows, kv_count, group_size, head_dim = q_grouped.shape
    k_rows = k_rot.shape[1]
    block_rows = q_rows
    while block_rows > 8 and n_batch * kv_count * group_size * block_rows * k_rows > 16777216:
        block_rows = block_rows // 2
    key_index = jnp.arange(k_rows)
    key_valid = key_index[None, :] < lengths[:, None]
    score_scale = head_dim ** -0.5

    def one_block(block_idx, out_buf):
        first_row = block_idx * block_rows
        q_block = lax.dynamic_slice_in_dim(q_grouped, first_row, block_rows, axis=1)
        scores = jnp.einsum('bqgrd,bkgd->bgrqk', q_block, k_rot, preferred_element_type=jnp.float32) * score_scale
        query_index = row_start + first_row + jnp.arange(block_rows)
        allowed = (key_index[None, :] <= query_index[:, None])[None, :, :] & key_valid[:, None, :]
        scores = jnp.where(allowed[:, None, None, :, :], scores, -1e30)
        attn_probs = jax.nn.softmax(scores, axis=-1).astype(jnp.bfloat16)
        block_out = jnp.einsum('bgrqk,bkgd->bqgrd', attn_probs, v_proj, preferred_element_type=jnp.float32)
        block_out = block_out.astype(jnp.bfloat16).reshape(n_batch, block_rows, kv_count * group_size * head_dim)
        return lax.dynamic_update_slice_in_dim(out_buf, block_out, first_row, axis=1)

    out_init = jnp.zeros((n_batch, q_rows, kv_count * group_size * head_dim), jnp.bfloat16)
    return lax.fori_loop(0, q_rows // block_rows, one_block, out_init)


def branches(normed, attn_out, w_o, w_gate, w_up, w_down):
    gate_proj = jnp.dot(normed, w_gate, preferred_element_type=jnp.float32)
    up_proj = jnp.dot(normed, w_up, preferred_element_type=jnp.float32)
    mlp_act = (jax.nn.silu(gate_proj) * up_proj).astype(jnp.bfloat16)
    return jnp.dot(attn_out, w_o, preferred_element_type=jnp.float32) + jnp.dot(mlp_act, w_down, preferred_element_type=jnp.float32)


def solution(mesh):
    act_spec = P('dp', None, None)
    col_spec = P(None, None, 'tp')
    row_spec = P(None, 'tp', None)
    cache_spec = P(None, 'dp', None, 'tp', None)
    in_specs = (act_spec, P('dp', None), P('dp'), col_spec, col_spec, col_spec, row_spec, col_spec, col_spec, row_spec, P(None, None), row_spec, row_spec)

    def device_body(x, positions, lengths, w_q, w_k, w_v, w_o, w_gate, w_up, w_down, norm_gain, q_gain, k_gain):
        cos_table, sin_table = rope_tables(positions)
        hidden = x
        k_list = []
        v_list = []
        for layer_idx in range(w_q.shape[0]):
            normed, q_grouped, k_rot, v_proj = project(hidden, cos_table, sin_table, w_q[layer_idx], w_k[layer_idx], w_v[layer_idx], norm_gain[layer_idx], q_gain[layer_idx], k_gain[layer_idx])
            attn_out = attend(q_grouped, k_rot, v_proj, lengths, 0)
            part_sum = branches(normed, attn_out, w_o[layer_idx], w_gate[layer_idx], w_up[layer_idx], w_down[layer_idx])
            full_sum = lax.psum(part_sum.astype(jnp.bfloat16), 'tp')
            hidden = (hidden.astype(jnp.float32) + full_sum.astype(jnp.float32)).astype(jnp.bfloat16)
            k_list.append(k_rot)
            v_list.append(v_proj)
        return hidden, jnp.stack(k_list), jnp.stack(v_list)

    return jax.shard_map(device_body, mesh=mesh, in_specs=in_specs, out_specs=(act_spec, cache_spec, cache_spec), check_vma=False)
```

profile of v0, /device:TPU:0, one launch (start us, length us, event | category | flops | bytes accessed | tf_op | source)
XLA Modules:
  0.0 995.6 jit_solution(11879306958104652529)
XLA Ops:
  7.2 1.3 iota_compare_fusion
  8.5 9.1 convert_reduce_fusion.1
  18.3 5.5 fusion.7
  24.5 3.6 slice_bitcast_fusion
  28.1 6.4 copy.86
  34.5 16.0 %fusion.104 = (f32[2,1024,4]{1,2,0:T(4,128)S(1)}, f32[2,1024,4,128]{1,3,2,0:T(8,128)}) fusion(bf16[4,128,4096,1]{2,1,0,3:T(8,128)(2,1)} %bitcast.181, f32[4096]{0:T(1024)S(1)} %bitcast.197, f32[2,1024]{1,0:T(2,128)S(1)} %add_rsqrt_fusion.5, f32[2,1024]{1,0:T(2,128)S(1)} %broadcast_multiply_fusion.5, bf16[2,1024,4096]{2,1,0:T(8,128)(2,1)} %param.13), kind=kOutput, calls=%fused_computation.151 | convolution fusion | flops 8632918016 | bytes 25231360 | tf_op jit(solution)/shard_map/dot_general | solution.py:38
  50.6 2.8 multiply_reduce_fusion.1
  54.0 2.9 multiply_multiply_fusion.1
  56.9 4.6 copy.129
  61.6 8.8 fusion.105
  71.3 1.2 slice_bitcast_fusion.4
  73.5 2.1 multiply_cosine_fusion
  75.6 2.4 fusion.76
  78.1 1.3 copy.85
  80.2 7.7 convolution_convert_fusion.1
  87.8 40.3 %fusion.34 = f32[2,1024,1792]{2,1,0:T(8,128)} fusion(bf16[2,4096,1792]{2,1,0:T(8,128)(2,1)} %param.20, bf16[2,1024,4096]{2,1,0:T(8,128)(2,1)} %param.13, f32[4096]{0:T(1024)} %bitcast.200, f32[2,1024]{1,0:T(2,128)} %copy-done.27, f32[2,1024]{1,0:T(2,128)S(1)} %copy-done.19), kind=kOutput, calls=%fused_computation.48 | convolution fusion | flops 30106714112 | bytes 46170112 | tf_op jit(solution)/shard_map/dot_general | solution.py:74
  128.1 40.2 %fusion.32 = f32[2,1024,1792]{2,1,0:T(8,128)} fusion(bf16[2,4096,1792]{2,1,0:T(8,128)(2,1)} %param.21, bf16[2,1024,4096]{2,1,0:T(8,128)(2,1)} %param.13, f32[4096]{0:T(1024)S(1)} %bitcast.201, f32[2,1024]{1,0:T(2,128)S(1)} %copy-done.28, f32[2,1024]{1,0:T(2,128)S(1)} %copy-done.19), kind=kOutput, calls=%fused_computation.46 | convolution fusion | flops 30106714112 | bytes 46170112 | tf_op jit(solution)/shard_map/dot_general | solution.py:75
  168.3 1.3 subtract_convert_fusion.1
  169.6 1.4 pad_maximum_fusion
  171.0 2.2 broadcast_and_fusion
  173.2 16.5 %fusion.14 = (f32[2,4,1024]{2,1,0:T(4,128)S(1)}, f32[2,1024,1024,4]{2,1,3,0:T(8,128)}) fusion(pred[2,1024,1024]{1,2,0:T(8,128)(4,1)S(1)} %broadcast_and_fusion, bf16[2,1024,4,128]{1,2,3,0:T(4,128)(2,1)S(1)} %bitcast.184, bf16[2,1024,128,1]{1,0,2,3:T(2,128)(2,1)} %bitcast.186), kind=kOutput, calls=%fused_computation.28 | convolution fusion | flops 2172641280 | bytes 38305792 | tf_op jit(solution)/shard_map/while/body/eval_jaxpr/bqgrd,bkgd->bgrqk/dot_general | solution.py:60
  189.7 14.4 %fusion.12 = f32[2,4,1024]{2,1,0:T(4,128)S(1)} fusion(f32[2,1024,1024,4]{2,1,3,0:T(8,128)} %get-tuple-element.92, f32[2,4,1024]{2,1,0:T(4,128)S(1)} %get-tuple-element.91, pred[2,1024,1024]{1,2,0:T(8,128)(4,1)S(1)} %broadcast_and_fusion), kind=kLoop, calls=%fused_computation.26 | loop fusion | flops 33546240 | bytes 35717120 | tf_op jit(solution)/shard_map/while/body/eval_jaxpr/reduce_sum | solution.py:64
  204.2 16.8 %fusion.52 = bf16[2,128,4,1024]{3,1,2,0:T(8,128)(2,1)} fusion(f32[2,4,1024]{2,1,0:T(4,128)S(1)} %fusion.12, f32[2,4,1024]{2,1,0:T(4,128)S(1)} %get-tuple-element.91, f32[2,1024,1024,4]{2,1,3,0:T(8,128)} %get-tuple-element.92, pred[2,1024,1024]{1,2,0:T(8,128)(4,1)S(1)} %broadcast_and_fusion, bf16[2,1024,128]{2,1,0:T(8,128)(2,1)S(1)} %copy-done.13), kind=kOutput, calls=%fused_computation.82 | convolution fusion | flops 2190475264 | bytes 38338560 | tf_op jit(solution)/shard_map/while/body/eval_jaxpr/bgrqk,bkgd->bqgrd/dot_general | solution.py:65
  221.0 41.3 %fusion.30 = f32[2,1024,4096]{2,1,0:T(8,128)} fusion(bf16[2,1792,4096]{2,1,0:T(8,128)(2,1)} %param.22, f32[2,1024,1792]{2,1,0:T(8,128)} %fusion.32, f32[2,1024,1792]{2,1,0:T(8,128)} %fusion.34), kind=kOutput, calls=%fused_computation.44 | convolution fusion | flops 30086791168 | bytes 77594624 | tf_op jit(solution)/shard_map/dot_general | solution.py:77
  262.3 20.3 %add_convert_fusion.1 = bf16[2,1024,4096]{2,1,0:T(8,128)(2,1)} fusion(f32[2,1024,4096]{2,1,0:T(8,128)} %fusion.30, bf16[2,1024,512]{1,2,0:T(8,128)(2,1)S(1)} %bitcast.203, bf16[2,512,4096]{2,1,0:T(8,128)(2,1)} %param.19), kind=kOutput, calls=%fused_computation.23 | convolution fusion | flops 8606711808 | bytes 56623104 | tf_op jit(solution)/shard_map/dot_general | solution.py:77
  282.6 6.4 copy.99
  289.1 213.8 %all-reduce.3.cloned.1.call-done = bf16[2,1024,4096]{2,1,0:T(8,128)(2,1)} async-done(((bf16[2,1024,4096]{2,1,0:T(8,128)(2,1)}), bf16[2,1024,4096]{2,1,0:T(8,128)(2,1)}) %all-reduce.3.cloned.1.call-update) | async-done | bytes 16777232 | tf_op jit(solution)/shard_map/psum | solution.py:96
  502.9 14.1 %convert_reduce_fusion = (f32[2,1024]{1,0:T(2,128)S(1)}, bf16[2,1024,4096]{2,1,0:T(8,128)(2,1)S(1)}) fusion(bf16[2,1024,4096]{2,1,0:T(8,128)(2,1)} %all-reduce.3.cloned.1.call-done, bf16[2,1024,4096]{2,1,0:T(8,128)(2,1)} %param.13), kind=kLoop, calls=%fused_computation.2 | loop fusion | flops 50329600 | bytes 50339840 | tf_op jit(solution)/shard_map/reduce_sum | solution.py:13
  517.0 5.7 fusion.4
  523.3 6.4 convolution_convert_fusion
  529.7 8.8 fusion.107
  538.5 41.1 %fusion.28 = f32[2,1024,1792]{2,1,0:T(8,128)} fusion(bf16[2,4096,1792]{2,1,0:T(8,128)(2,1)} %param.20, bf16[2,1024,4096]{2,1,0:T(8,128)(2,1)} %copy-done, f32[4096]{0:T(1024)} %bitcast.193, f32[2,1024]{1,0:T(2,128)} %copy-done.29, f32[2,1024]{1,0:T(2,128)S(1)} %broadcast_multiply_fusion.4), kind=kOutput, calls=%fused_computation.42 | convolution fusion | flops 30106714112 | bytes 46170112 | tf_op jit(solution)/shard_map/dot_general | solution.py:74
  579.7 40.1 %fusion.26 = f32[2,1024,1792]{2,1,0:T(8,128)} fusion(bf16[2,4096,1792]{2,1,0:T(8,128)(2,1)} %param.21, bf16[2,1024,4096]{2,1,0:T(8,128)(2,1)} %copy-done, f32[4096]{0:T(1024)S(1)} %bitcast.195, f32[2,1024]{1,0:T(2,128)S(1)} %copy-done.30, f32[2,1024]{1,0:T(2,128)S(1)} %broadcast_multiply_fusion.4), kind=kOutput, calls=%fused_computation.40 | convolution fusion | flops 30106714112 | bytes 46170112 | tf_op jit(solution)/shard_map/dot_general | solution.py:75
  621.1 2.4 fusion.78
  624.1 13.2 %fusion.106 = (f32[2,1024,4]{1,2,0:T(4,128)S(1)}, f32[2,1024,4,128]{1,3,2,0:T(8,128)S(1)}) fusion(bf16[4,128,4096,1]{2,1,0,3:T(8,128)(2,1)S(1)} %bitcast.180, f32[4096]{0:T(1024)S(1)} %bitcast.196, f32[2,1024]{1,0:T(2,128)S(1)} %copy-done.30, f32[2,1024]{1,0:T(2,128)S(1)} %broadcast_multiply_fusion.4, bf16[2,1024,4096]{2,1,0:T(8,128)(2,1)} %copy-done), kind=kOutput, calls=%fused_computation.153 | convolution fusion | flops 8632918016 | bytes 25231360 | tf_op jit(solution)/shard_map/dot_general | solution.py:38
  638.7 2.7 copy.130
  641.4 1.2 subtract_convert_fusion
  642.6 1.4 pad_maximum_fusion.1
  644.0 14.7 %fusion.15 = (f32[2,4,1024]{2,1,0:T(4,128)S(1)}, f32[2,1024,1024,4]{2,1,3,0:T(8,128)}) fusion(pred[2,1024,1024]{1,2,0:T(8,128)(4,1)S(1)} %copy-done.3, bf16[2,1024,4,128]{1,2,3,0:T(4,128)(2,1)S(1)} %bitcast.185, bf16[2,1024,128,1]{1,0,2,3:T(2,128)(2,1)S(1)} %bitcast.188), kind=kOutput, calls=%fused_computation.29 | convolution fusion | flops 2172641280 | bytes 38305792 | tf_op jit(solution)/shard_map/while/body/eval_jaxpr/bqgrd,bkgd->bgrqk/dot_general | solution.py:60
  658.7 14.4 %fusion.13 = f32[2,4,1024]{2,1,0:T(4,128)S(1)} fusion(f32[2,1024,1024,4]{2,1,3,0:T(8,128)} %get-tuple-element.98, f32[2,4,1024]{2,1,0:T(4,128)S(1)} %get-tuple-element.97, pred[2,1024,1024]{1,2,0:T(8,128)(4,1)S(1)} %copy-done.3), kind=kLoop, calls=%fused_computation.27 | loop fusion | flops 33546240 | bytes 35717120 | tf_op jit(solution)/shard_map/while/body/eval_jaxpr/reduce_sum | solution.py:64
  673.2 16.7 %fusion.55 = bf16[2,128,4,1024]{3,1,2,0:T(8,128)(2,1)} fusion(f32[2,4,1024]{2,1,0:T(4,128)S(1)} %fusion.13, f32[2,4,1024]{2,1,0:T(4,128)S(1)} %get-tuple-element.97, f32[2,1024,1024,4]{2,1,3,0:T(8,128)} %get-tuple-element.98, pred[2,1024,1024]{1,2,0:T(8,128)(4,1)S(1)} %copy-done.3, bf16[2,1024,128]{2,1,0:T(8,128)(2,1)S(1)} %copy-done.15), kind=kOutput, calls=%fused_computation.83 | convolution fusion | flops 2190475264 | bytes 38338560 | tf_op jit(solution)/shard_map/while/body/eval_jaxpr/bgrqk,bkgd->bqgrd/dot_general | solution.py:65
  689.9 41.3 %fusion.24 = f32[2,1024,4096]{2,1,0:T(8,128)} fusion(bf16[2,1792,4096]{2,1,0:T(8,128)(2,1)} %param.22, f32[2,1024,1792]{2,1,0:T(8,128)} %fusion.26, f32[2,1024,1792]{2,1,0:T(8,128)} %fusion.28), kind=kOutput, calls=%fused_computation.38 | convolution fusion | flops 30086791168 | bytes 77594624 | tf_op jit(solution)/shard_map/dot_general | solution.py:77
  731.2 20.5 %add_convert_fusion = bf16[2,1024,4096]{2,1,0:T(8,128)(2,1)} fusion(f32[2,1024,4096]{2,1,0:T(8,128)} %fusion.24, bf16[2,1024,512]{1,2,0:T(8,128)(2,1)S(1)} %bitcast.202, bf16[2,512,4096]{2,1,0:T(8,128)(2,1)} %param.19), kind=kOutput, calls=%fused_computation.20 | convolution fusion | flops 8606711808 | bytes 56623104 | tf_op jit(solution)/shard_map/dot_general | solution.py:77
  752.8 1.5 pad_maximum_fusion.2
  754.3 2.1 copy.109
  756.4 1.1 maximum_bitcast_fusion
  757.5 211.7 %all-reduce.5.cloned.1.call-done = bf16[2,1024,4096]{2,1,0:T(8,128)(2,1)} async-done(((bf16[2,1024,4096]{2,1,0:T(8,128)(2,1)}), bf16[2,1024,4096]{2,1,0:T(8,128)(2,1)}) %all-reduce.5.cloned.1.call-update) | async-done | bytes 16777232 | tf_op jit(solution)/shard_map/psum | solution.py:96
  969.2 19.3 %fusion.11 = bf16[2,1024,4096]{2,1,0:T(8,128)(2,1)} fusion(bf16[2,1024,4096]{2,1,0:T(8,128)(2,1)} %copy-done, bf16[2,1024,4096]{2,1,0:T(8,128)(2,1)} %all-reduce.5.cloned.1.call-done), kind=kLoop, calls=%fused_computation.17 | loop fusion | flops 33554432 | bytes 50331648 | tf_op jit(solution)/shard_map/convert_element_type | solution.py:97
  (126 shorter events, 9.7 us)
Async XLA Ops:
  7.2 495.7 %all-reduce.3.cloned.1.call-start = ((), (), s32[]{:S(2)}) async-start(), calls=%async_computation | async-start | bytes 33554432 | tf_op jit(solution)/shard_map/psum | solution.py:96
  7.2 11.0 %copy-start.1 = (bf16[2,1024,4096]{2,1,0:T(8,128)(2,1)S(1)}, bf16[2,1024,4096]{2,1,0:T(8,128)(2,1)}, u32[]{:S(2)}) copy-start(bf16[2,1024,4096]{2,1,0:T(8,128)(2,1)} %param.13) | copy-start | bytes 50331652
  7.2 68.4 %copy-start.32 = (f32[64]{0:T(128)}, f32[64]{0:T(128)S(1)}, u32[]{:S(2)}) copy-start(f32[64]{0:T(128)S(1)} %negate_power_fusion) | copy-start | bytes 772
  8.5 15.3 %copy-start.20 = (f32[2,4096]{1,0:T(2,128)S(1)}, f32[2,4096]{1,0:T(2,128)}, u32[]{:S(2)}) copy-start(f32[2,4096]{1,0:T(2,128)} %param.23) | copy-start | bytes 98308
  8.5 15.9 %slice-start.4 = ((s8[8388608]{0:T(1024)(128)(4,1)}), s8[4194304]{0:T(1024)(128)(4,1)S(1)}, s32[]{:S(2)}) async-start(s8[8388608]{0:T(1024)(128)(4,1)} %bitcast.178), calls=%async_computation.6 | async-start | bytes 8388608
  18.3 16.2 %copy-start.18 = (f32[2,1024]{1,0:T(2,128)}, f32[2,1024]{1,0:T(2,128)S(1)}, u32[]{:S(2)}) copy-start(f32[2,1024]{1,0:T(2,128)S(1)} %broadcast_multiply_fusion.5) | copy-start | bytes 24580
  18.3 6.2 slice-start.5
  23.8 26.7 %copy-start.27 = (f32[2,1024]{1,0:T(2,128)}, f32[2,1024]{1,0:T(2,128)S(1)}, u32[]{:S(2)}) copy-start(f32[2,1024]{1,0:T(2,128)S(1)} %add_rsqrt_fusion.5) | copy-start | bytes 24580
  24.5 26.1 %copy-start.23 = (f32[1,4096]{1,0:T(1,128)}, f32[1,4096]{1,0:T(1,128)S(1)}, u32[]{:S(2)}) copy-start(f32[1,4096]{1,0:T(1,128)S(1)} %get-tuple-element.80) | copy-start | bytes 49156
  34.5 27.1 %slice-start = ((s8[16777216]{0:T(1024)(128)(4,1)}), s8[4194304]{0:T(1024)(128)(4,1)S(1)}, s32[]{:S(2)}) async-start(s8[16777216]{0:T(1024)(128)(4,1)} %bitcast.174), calls=%async_computation.2 | async-start | bytes 8388608
  34.5 18.9 %copy-start.34 = (f32[2,4,128]{2,1,0:T(4,128)S(1)}, f32[2,4,128]{2,1,0:T(4,128)}, u32[]{:S(2)}) copy-start(f32[2,4,128]{2,1,0:T(4,128)} %param.24) | copy-start | bytes 12292
  34.5 27.1 %slice-start.1 = ((s8[16777216]{0:T(1024)(128)(4,1)}), s8[4194304]{0:T(1024)(128)(4,1)S(1)}, s32[]{:S(2)}) async-start(s8[16777216]{0:T(1024)(128)(4,1)} %bitcast.174), calls=%async_computation.3 | async-start | bytes 8388608
  34.5 27.1 %slice-start.2 = ((s8[16777216]{0:T(1024)(128)(4,1)}), s8[4194304]{0:T(1024)(128)(4,1)S(1)}, s32[]{:S(2)}) async-start(s8[16777216]{0:T(1024)(128)(4,1)} %bitcast.174), calls=%async_computation.4 | async-start | bytes 8388608
  34.5 27.1 %slice-start.3 = ((s8[16777216]{0:T(1024)(128)(4,1)}), s8[4194304]{0:T(1024)(128)(4,1)S(1)}, s32[]{:S(2)}) async-start(s8[16777216]{0:T(1024)(128)(4,1)} %bitcast.174), calls=%async_computation.5 | async-start | bytes 8388608
  50.6 11.0 %copy-start.26 = (s32[2,1024]{1,0:T(2,128)S(1)}, s32[2,1024]{1,0:T(2,128)}, u32[]{:S(2)}) copy-start(s32[2,1024]{1,0:T(2,128)} %param.14) | copy-start | bytes 24580
  61.6 14.0 %copy-start.16 = (f32[2,1024]{1,0:T(2,128)}, f32[2,1024]{1,0:T(2,128)S(1)}, u32[]{:S(2)}) copy-start(f32[2,1024]{1,0:T(2,128)S(1)} %convert_element_type.124) | copy-start | bytes 24580
  75.6 92.7 %copy-start.5 = (f32[2,1024,64]{1,2,0:T(8,128)}, f32[2,1024,64]{1,2,0:T(8,128)S(1)}, u32[]{:S(2)}) copy-start(f32[2,1024,64]{1,2,0:T(8,128)S(1)} %get-tuple-element.81) | copy-start | bytes 1572868
  75.6 92.7 %copy-start.7 = (f32[2,1024,64]{1,2,0:T(8,128)}, f32[2,1024,64]{1,2,0:T(8,128)S(1)}, u32[]{:S(2)}) copy-start(f32[2,1024,64]{1,2,0:T(8,128)S(1)} %get-tuple-element.82) | copy-start | bytes 1572868
  80.2 7.7 copy-start.19
  87.8 40.3 %copy-start.24 = (f32[1,4096]{1,0:T(1,128)S(1)}, f32[1,4096]{1,0:T(1,128)}, u32[]{:S(2)}) copy-start(f32[1,4096]{1,0:T(1,128)} %copy-done.23) | copy-start | bytes 49156
  87.8 40.3 %copy-start.28 = (f32[2,1024]{1,0:T(2,128)S(1)}, f32[2,1024]{1,0:T(2,128)}, u32[]{:S(2)}) copy-start(f32[2,1024]{1,0:T(2,128)} %copy-done.27) | copy-start | bytes 24580
  128.1 40.2 %copy-start.4 = (f32[2,1024,4,128]{1,2,3,0:T(4,128)S(1)}, f32[2,1024,4,128]{1,2,3,0:T(4,128)}, u32[]{:S(2)}) copy-start(f32[2,1024,4,128]{1,2,3,0:T(4,128)} %copy.129) | copy-start | bytes 12582916
  173.2 30.9 %copy-start.2 = (pred[2,1024,1024]{1,2,0:T(8,128)(4,1)}, pred[2,1024,1024]{1,2,0:T(8,128)(4,1)S(1)}, u32[]{:S(2)}) copy-start(pred[2,1024,1024]{1,2,0:T(8,128)(4,1)S(1)} %broadcast_and_fusion) | copy-start | bytes 6291460
  189.7 14.4 %copy-start.13 = (bf16[2,1024,128]{2,1,0:T(8,128)(2,1)S(1)}, bf16[2,1024,128]{2,1,0:T(8,128)(2,1)}, u32[]{:S(2)}) copy-start(bf16[2,1024,128]{2,1,0:T(8,128)(2,1)} %convolution_convert_fusion.1) | copy-start | bytes 1572868
  221.0 41.3 %copy-start.38 = (bf16[2,128,4,1024]{3,1,2,0:T(8,128)(2,1)S(1)}, bf16[2,128,4,1024]{3,1,2,0:T(8,128)(2,1)}, u32[]{:S(2)}) copy-start(bf16[2,128,4,1024]{3,1,2,0:T(8,128)(2,1)} %fusion.52) | copy-start | bytes 6291460
  282.6 686.6 %all-reduce.5.cloned.1.call-start = ((), (), s32[]{:S(2)}) async-start(), calls=%async_computation.1 | async-start | bytes 33554432 | tf_op jit(solution)/shard_map/psum | solution.py:96
  516.9 12.8 %copy-start = (bf16[2,1024,4096]{2,1,0:T(8,128)(2,1)}, bf16[2,1024,4096]{2,1,0:T(8,128)(2,1)S(1)}, u32[]{:S(2)}) copy-start(bf16[2,1024,4096]{2,1,0:T(8,128)(2,1)S(1)} %get-tuple-element.64) | copy-start | bytes 50331652
  516.9 6.4 copy-start.21
  516.9 6.4 copy-start.36
  522.7 0.6 copy-start.29
  538.5 41.1 %copy-start.22 = (f32[1,4096]{1,0:T(1,128)S(1)}, f32[1,4096]{1,0:T(1,128)}, u32[]{:S(2)}) copy-start(f32[1,4096]{1,0:T(1,128)} %get-tuple-element.79) | copy-start | bytes 49156
  538.5 41.1 %copy-start.30 = (f32[2,1024]{1,0:T(2,128)S(1)}, f32[2,1024]{1,0:T(2,128)}, u32[]{:S(2)}) copy-start(f32[2,1024]{1,0:T(2,128)} %copy-done.29) | copy-start | bytes 24580
  579.7 40.1 %copy-start.31 = (f32[2,1024]{1,0:T(2,128)S(1)}, f32[2,1024]{1,0:T(2,128)}, u32[]{:S(2)}) copy-start(f32[2,1024]{1,0:T(2,128)} %get-tuple-element.95) | copy-start | bytes 24580
  579.7 40.3 %copy-start.35 = (f32[128]{0:T(128)S(1)}, f32[128]{0:T(128)}, u32[]{:S(2)}) copy-start(f32[128]{0:T(128)} %get-tuple-element.85) | copy-start | bytes 1540
  579.7 41.3 %copy-start.17 = (f32[2,1024]{1,0:T(2,128)S(1)}, f32[2,1024]{1,0:T(2,128)}, u32[]{:S(2)}) copy-start(f32[2,1024]{1,0:T(2,128)} %copy-done.16) | copy-start | bytes 24580
  579.7 41.3 %copy-start.33 = (f32[64]{0:T(128)S(1)}, f32[64]{0:T(128)}, u32[]{:S(2)}) copy-start(f32[64]{0:T(128)} %copy-done.32) | copy-start | bytes 772
  579.7 44.4 %copy-start.9 = (bf16[512,4096]{1,0:T(8,128)(2,1)S(1)}, bf16[512,4096]{1,0:T(8,128)(2,1)}, u32[]{:S(2)}) copy-start(bf16[512,4096]{1,0:T(8,128)(2,1)} %copy.99) | copy-start | bytes 12582916
  624.1 19.9 %copy-start.11 = (bf16[2,1024,1,64,2]{1,0,4,3,2:T(2,128)(2,1)}, bf16[2,1024,1,64,2]{1,0,4,3,2:T(2,128)(2,1)S(1)}, u32[]{:S(2)}) copy-start(bf16[2,1024,1,64,2]{1,0,4,3,2:T(2,128)(2,1)S(1)} %copy.98) | copy-start | bytes 1572868
  624.1 13.9 %copy-start.25 = (f32[4,128]{1,0:T(4,128)S(1)}, f32[4,128]{1,0:T(4,128)}, u32[]{:S(2)}) copy-start(f32[4,128]{1,0:T(4,128)} %get-tuple-element.83) | copy-start | bytes 6148
  637.3 4.1 copy-start.6
  637.3 4.1 copy-start.8
  637.3 6.7 copy-start.3
  658.7 14.4 %copy-start.15 = (bf16[2,1024,128]{2,1,0:T(8,128)(2,1)S(1)}, bf16[2,1024,128]{2,1,0:T(8,128)(2,1)}, u32[]{:S(2)}) copy-start(bf16[2,1024,128]{2,1,0:T(8,128)(2,1)} %convolution_convert_fusion) | copy-start | bytes 1572868
  689.9 41.3 %copy-start.37 = (bf16[2,128,4,1024]{3,1,2,0:T(8,128)(2,1)S(1)}, bf16[2,128,4,1024]{3,1,2,0:T(8,128)(2,1)}, u32[]{:S(2)}) copy-start(bf16[2,128,4,1024]{3,1,2,0:T(8,128)(2,1)} %fusion.55) | copy-start | bytes 6291460
  751.6 1.0 copy-start.10
  751.6 1.2 copy-start.12
  751.7 4.8 copy-start.14
Sparse Core Ops, SparseCore 0:
  282.7 220.0 all-reduce.2
  751.8 217.3 all-reduce.4
where the time goes:
time: 1000 us; the launch traced here: 996 us
  waiting for transfers between devices  426 us (43%)
  matrix products  411 us (41%)
  other arithmetic  110 us (11%)
  local copies, waits for them, and re-layouts  34.4 us (3%)
  between operations  15 us (2%)
    psum x2, waiting for transfers between devices, device_body(): full_sum = lax.psum(part_sum.astype(jnp.bfloat16), 'tp')  425 us
    dot_general x2, matrix products, branches(): jnp.dot(mlp_act, w_down, preferred_element_type=jnp.float32)  82.6 us
    dot_general x2, matrix products, branches(): gate_proj = jnp.dot(normed, w_gate, preferred_element_type=jnp.float32)  81.4 us
    dot_general x2, matrix products, branches(): up_proj = jnp.dot(normed, w_up, preferred_element_type=jnp.float32)  80.3 us
    dot_general x2, matrix products, branches(): jnp.dot(attn_out, w_o, preferred_element_type=jnp.float32)  40.8 us
    dot_general x2, matrix products, one_block(): jnp.einsum('bgrqk,bkgd->bqgrd', attn_probs, v_proj, preferred_element_typ...  33.5 us
    dot_general x2, matrix products, one_block(): jnp.einsum('bqgrd,bkgd->bgrqk', q_block, k_rot, preferred_element_type=jn...  31.2 us
    dot_general x2, matrix products, project(): jnp.dot(normed, w_q, preferred_element_type=jnp.float32)  29.2 us
  transfers between devices with their start and end apart: 2, of which 2 were waited for; matrix products, arithmetic and copies ran while one was open for 1% of the time, Pallas kernels for 0%

commit v1 on v0

v1 whole, which is shorter than its diff:
```python
import functools
import math

import jax
import jax.numpy as jnp
from jax import lax
from jax.experimental import pallas as pl
from jax.experimental.pallas import tpu as pltpu
from jax.sharding import PartitionSpec as P

HEAD = 128
ROPE_THETA = 75000000.0
NORM_EPS = 1e-5
BF = jnp.bfloat16
F32 = jnp.float32
MESH = pl.DeviceIdType.MESH
NG = 4
KINDS = 9
D2D, S1, S2, A2, A1A, A1B, A0A, A0B, A0C = range(KINDS)

LN_EV = {0: [("s0", 3)], 1: [("s1", 0)], 3: [("s1", 1)]}
ATT_EV = {0: [("s1", 2), ("s2", 0)], 1: [("s1", 3), ("s2", 1)]}
GU_EV = {0: [("a2", 0), ("s2", 2)], 1: [("a2", 1), ("s2", 3)], 2: [("a1", 0)], 3: [("a2", 2)], 4: [("a1", 1), ("a2", 3)], 5: [("a1", 2)], 6: [("a1", 3)]}
TAIL_EV = [("s0", 3), ("s1", 0), ("s1", 1), ("s2", 0), ("s1", 2), ("s2", 1), ("a2", 0), ("s1", 3), ("s2", 2), ("a2", 1), ("a1", 0), ("s2", 3), ("a2", 2), ("a1", 1), ("a2", 3), ("a1", 2), ("a1", 3)]


def mo(v, m):
    return pl.multiple_of(v, m)


def mega(cfg, lens, x, cos, sin, wq, wk, wv, wo, wg, wu, wd, ng, qg, kg,
         hy, kc, vc,
         wqkv, wgu, wdn, nbuf, hblk, ou, pbuf, d2d, s1b, s2b, res, qkvf, qbuf, kbuf, vbuf, csb,
         ssem, rsem, wsem, lsem, osem):
    CH, D, F, NH, NC, HS = cfg["CH"], cfg["D"], cfg["F"], cfg["NH"], cfg["NC"], cfg["HS"]
    GC = D // NG
    FT = cfg["FT"]
    NT = F // FT
    OW = NH * HEAD
    LB = CH // 4
    QB = CH // 4
    tp = lax.axis_index("tp")
    core = lax.rem(tp, 2)
    bx = lax.rem(lax.div(tp, 2), 2)
    by = lax.div(tp, 4)
    xn = tp + 2 - 4 * bx
    yn = tp + 4 - 8 * by
    cn = tp + 1 - 2 * core
    n1 = jnp.where(core == 0, xn, yn)
    n2 = jnp.where(core == 0, yn, xn)
    b1 = jnp.where(core == 0, bx, by)
    b2 = jnp.where(core == 0, by, bx)
    H2, H4, H8 = CH // 2, CH // 4, CH // 8
    my_row = core * H2 + b1 * H4 + b2 * H8

    def where(c):
        l = lax.div(c, 2 * HS)
        b = lax.rem(lax.div(c, HS), 2)
        s = lax.rem(c, HS)
        return l, b, s

    def rcopy(kind, c, g, src, dst, dev):
        par = lax.rem(c, 2)
        return pltpu.make_async_remote_copy(
            src_ref=src, dst_ref=dst, send_sem=ssem.at[kind, par, g], recv_sem=rsem.at[kind, par, g],
            device_id={"tp": dev}, device_id_type=MESH)

    def hrows(c, off, n, g):
        l, b, s = where(c)
        return hy.at[l, b, pl.ds(mo(s * CH + off, H8), n), pl.ds(mo(g * GC, GC), GC)]

    def k_d2d(c, g):
        par = lax.rem(c, 2)
        return rcopy(D2D, c, g, pbuf.at[g, pl.ds(mo((1 - core) * H2, H2), H2)], d2d.at[par, g], cn)

    def k_s1(c, g):
        par = lax.rem(c, 2)
        return rcopy(S1, c, g, d2d.at[par, g, pl.ds(mo((1 - b1) * H4, H4), H4)], s1b.at[par, g], n1)

    def k_s2(c, g):
        par = lax.rem(c, 2)
        return rcopy(S2, c, g, s1b.at[par, g, pl.ds(mo((1 - b2) * H8, H8), H8)], s2b.at[par, g], n2)

    def k_own(kind, c, g, dev):
        return rcopy(kind, c, g, s2b.at[lax.rem(c, 2), g], hrows(c, my_row, H8, g), dev)

    def k_fwd(kind, c, g, dev):
        if kind == A0C:
            off, n = core * H2 + (1 - b1) * H4, H4
        else:
            off, n = core * H2 + b1 * H4 + (1 - b2) * H8, H8
        ref = hrows(c, off, n, g)
        return rcopy(kind, c, g, ref, ref, dev)

    def k_loc(c, g):
        return pltpu.make_async_copy(s2b.at[lax.rem(c, 2), g], hrows(c, my_row, H8, g), lsem.at[2 + lax.rem(c, 2), g])

    def c_res(c):
        l, b, s = where(c)
        rows = pl.ds(mo(s * CH + my_row, H8), H8)
        return (pltpu.make_async_copy(x.at[b, rows], res, lsem.at[1, 0]),
                pltpu.make_async_copy(hy.at[0, b, rows], res, lsem.at[1, 0]))

    RB = min(32, H8)

    def s0(c, g):
        par = lax.rem(c, 2)
        cp = k_d2d(c, g)
        cp.wait_recv()
        cp.wait_send()

        @pl.loop(0, H2 // RB)
        def _(r):
            rr = pl.ds(mo(r * RB, RB), RB)
            d2d[par, g, rr] = d2d[par, g, rr] + pbuf[g, pl.ds(mo(core * H2 + r * RB, RB), RB)]
        k_s1(c, g).start()

    def s1(c, g):
        par = lax.rem(c, 2)
        cp = k_s1(c, g)
        cp.wait_recv()
        cp.wait_send()

        @pl.loop(0, H4 // RB)
        def _(r):
            rr = pl.ds(mo(r * RB, RB), RB)
            s1b[par, g, rr] = s1b[par, g, rr] + d2d[par, g, pl.ds(mo(b1 * H4 + r * RB, RB), RB)]
        k_s2(c, g).start()

    def s2(c, g):
        par = lax.rem(c, 2)
        cp = k_s2(c, g)
        cp.wait_recv()
        cp.wait_send()
        if g == 0:
            c_res(c)[0].wait()

        @pl.loop(0, H8 // RB)
        def _(r):
            rr = pl.ds(mo(r * RB, RB), RB)
            t = s2b[par, g, rr].astype(F32) + s1b[par, g, pl.ds(mo(b2 * H8 + r * RB, RB), RB)].astype(F32)
            s2b[par, g, rr] = (t + res[rr, pl.ds(g * GC, GC)].astype(F32)).astype(BF)
        k_own(A2, c, g, n2).start()
        k_own(A1A, c, g, n1).start()
        k_own(A0A, c, g, cn).start()
        k_loc(c, g).start()

    def a2(c, g):
        cp = k_own(A2, c, g, n2)
        cp.wait_recv()
        cp.wait_send()
        k_fwd(A1B, c, g, n1).start()
        k_fwd(A0B, c, g, cn).start()

    def a1(c, g):
        for cp in (k_own(A1A, c, g, n1), k_fwd(A1B, c, g, n1)):
            cp.wait_recv()
            cp.wait_send()
        k_fwd(A0C, c, g, cn).start()

    def a0(c):
        for g in range(NG):
            for cp in (k_own(A0A, c, g, cn), k_fwd(A0B, c, g, cn), k_fwd(A0C, c, g, cn)):
                cp.wait_recv()
                cp.wait_send()
            k_loc(c, g).wait()

    handlers = {"s0": s0, "s1": s1, "s2": s2, "a2": a2, "a1": a1}

    def events(c, evs, extra=None):
        if evs:
            @pl.when(c >= 0 if extra is None else (c >= 0) & extra)
            def _():
                for name, g in evs:
                    handlers[name](c, g)

    def c_qkv(l):
        return (pltpu.make_async_copy(wq.at[l], wqkv.at[:, pl.ds(0, OW)], wsem.at[0, 0]),
                pltpu.make_async_copy(wk.at[l], wqkv.at[:, pl.ds(OW, HEAD)], wsem.at[0, 1]),
                pltpu.make_async_copy(wv.at[l], wqkv.at[:, pl.ds(OW + HEAD, HEAD)], wsem.at[0, 2]))

    def c_gu(l, j):
        sl = lax.rem(j, 2)
        cc = pl.ds(mo(j * FT, FT), FT)
        return (pltpu.make_async_copy(wg.at[l, :, cc], wgu.at[sl, :, pl.ds(0, FT)], wsem.at[1, sl]),
                pltpu.make_async_copy(wu.at[l, :, cc], wgu.at[sl, :, pl.ds(FT, FT)], wsem.at[2, sl]))

    def c_dn(l, g):
        sl = lax.rem(g, 2)
        cc = pl.ds(mo(g * GC, GC), GC)
        return (pltpu.make_async_copy(wo.at[l, :, cc], wdn.at[sl, pl.ds(0, OW)], wsem.at[3, sl]),
                pltpu.make_async_copy(wd.at[l, :, cc], wdn.at[sl, pl.ds(OW, F)], wsem.at[4, sl]))

    def c_h(c, r):
        l, b, s = where(c)
        sl = lax.rem(r, 2)
        rows = pl.ds(mo(s * CH + r * LB, LB), LB)
        return (pltpu.make_async_copy(x.at[b, rows], hblk.at[sl], lsem.at[0, sl]),
                pltpu.make_async_copy(hy.at[0, b, rows], hblk.at[sl], lsem.at[0, sl]))

    def c_cs(c):
        l, b, s = where(c)
        rows = pl.ds(mo(s * CH, CH), CH)
        return (pltpu.make_async_copy(cos.at[b, rows], csb.at[0], wsem.at[5, 0]),
                pltpu.make_async_copy(sin.at[b, rows], csb.at[1], wsem.at[5, 1]))

    def c_kv(c):
        l, b, s = where(c)
        rows = pl.ds(mo(s * CH, CH), CH)
        return (pltpu.make_async_copy(kbuf.at[rows], kc.at[l, b, rows], osem.at[0]),
                pltpu.make_async_copy(vbuf.at[rows], vc.at[l, b, rows], osem.at[1]))

    def start(cps):
        for cp in cps:
            cp.start()

    def wait(cps):
        for cp in cps:
            cp.wait()

    def start_by_layer(c, pair):
        @pl.when(c < 2 * HS)
        def _():
            pair[0].start()

        @pl.when(c >= 2 * HS)
        def _():
            pair[1].start()

    bar = pltpu.get_barrier_semaphore()
    for dev in (xn, yn, cn):
        pl.semaphore_signal(bar, inc=1, device_id={"tp": dev}, device_id_type=MESH)

    start(c_qkv(0))
    c_h(0, 0)[0].start()
    start(c_cs(0))
    pl.semaphore_wait(bar, 3)

    @pl.loop(0, NC)
    def _(i):
        l, b, s = where(i)
        c = i - 1

        @pl.when(i >= 2)
        def _():
            a0(i - 2)

        gain = ng[pl.ds(l, 1), :]

        @pl.loop(0, CH // LB)
        def _(r):
            c_h(i, r)[0].wait()

            @pl.when(r + 1 < CH // LB)
            def _():
                start_by_layer(i, c_h(i, r + 1))
            for k, evs in LN_EV.items():
                events(c, evs, r == k)
            sl = lax.rem(r, 2)

            @pl.loop(0, LB // 16)
            def _(q):
                v = hblk[sl, pl.ds(mo(q * 16, 16), 16), :].astype(F32)
                mean = jnp.sum(v, axis=1, keepdims=True) * (1.0 / D)
                v = v - mean
                var = jnp.sum(v * v, axis=1, keepdims=True) * (1.0 / D)
                nbuf[pl.ds(mo(r * LB + q * 16, 16), 16), :] = (v * lax.rsqrt(var + NORM_EPS) * gain).astype(BF)

        wait(c_qkv(l))
        start(c_gu(l, 0))

        @pl.when(i > 0)
        def _():
            wait(c_kv(i - 1))
        qkvf[...] = jnp.dot(nbuf[...], wqkv[...], preferred_element_type=F32)
        wait(c_cs(i))
        lane = lax.broadcasted_iota(jnp.int32, (64, HEAD), 1)
        even = lax.rem(lane, 2) == 0

        @pl.loop(0, CH // 64)
        def _(r):
            rr = pl.ds(mo(r * 64, 64), 64)
            ct = csb[0, rr]
            st = csb[1, rr]

            def norm_rope(v, gvec):
                mean = jnp.sum(v, axis=1, keepdims=True) * (1.0 / HEAD)
                v = v - mean
                var = jnp.sum(v * v, axis=1, keepdims=True) * (1.0 / HEAD)
                v = v * lax.rsqrt(var + NORM_EPS) * gvec
                sw = jnp.where(even, pltpu.roll(v, HEAD - 1, 1), pltpu.roll(v, 1, 1))
                return (v * ct + sw * st).astype(BF)
            for h in range(NH):
                qbuf[h, rr] = norm_rope(qkvf[rr, pl.ds(h * HEAD, HEAD)], qg[l, pl.ds(h, 1), :])
            ks = pl.ds(mo(s * CH + r * 64, 64), 64)
            kbuf[ks] = norm_rope(qkvf[rr, pl.ds(OW, HEAD)], kg[l])
            vbuf[ks] = qkvf[rr, pl.ds(OW + HEAD, HEAD)].astype(BF)

        start(c_kv(i))

        @pl.when(i + 1 < NC)
        def _():
            start(c_cs(i + 1))
        rlen = lens[b]
        scale = HEAD ** -0.5

        def attn(s_static, qb):
            base = s_static * CH + qb * QB
            nk = base + QB
            q4 = qbuf[:, pl.ds(qb * QB, QB), :].reshape(NH * QB, HEAD)
            sc = lax.dot_general(q4, kbuf[pl.ds(0, nk)], (((1,), (1,)), ((), ())), preferred_element_type=F32)
            kid = lax.broadcasted_iota(jnp.int32, (QB, nk), 1)
            qid = lax.broadcasted_iota(jnp.int32, (QB, nk), 0) + base
            bias = jnp.where((kid <= qid) & (kid < rlen), 0.0, -1e30)
            sc = sc.reshape(NH, QB, nk) * scale + bias[None]
            m = jnp.max(sc, axis=2, keepdims=True)
            e = jnp.exp(sc - m)
            pr = (e * (1.0 / jnp.sum(e, axis=2, keepdims=True))).astype(BF)
            o = jnp.dot(pr.reshape(NH * QB, nk), vbuf[pl.ds(0, nk)], preferred_element_type=F32).astype(BF)
            for h in range(NH):
                ou[pl.ds(qb * QB, QB), pl.ds(h * HEAD, HEAD)] = o[h * QB:(h + 1) * QB]

        for half in range(2):
            events(c, ATT_EV.get(half))
            for ss in range(HS):
                @pl.when(s == ss)
                def _():
                    for qb in range(half * 2, half * 2 + 2):
                        attn(ss, qb)

        @pl.loop(0, NT)
        def _(j):
            wait(c_gu(l, j))

            @pl.when(j + 1 < NT)
            def _():
                start(c_gu(l, j + 1))

            @pl.when(j + 1 == NT)
            def _():
                start(c_dn(l, 0))
            for k, evs in GU_EV.items():
                events(c, evs, j == min(k, NT - 1))
            r = jnp.dot(nbuf[...], wgu[lax.rem(j, 2)], preferred_element_type=F32)
            ou[:, pl.ds(mo(OW + j * FT, 128), FT)] = (jax.nn.silu(r[:, :FT]) * r[:, FT:]).astype(BF)

        @pl.when(i + 1 < NC)
        def _():
            start(c_qkv(where(i + 1)[0]))
            start_by_layer(i + 1, c_h(i + 1, 0))
        start_by_layer(i, c_res(i))

        @pl.loop(0, NG)
        def _(g):
            wait(c_dn(l, g))

            @pl.when(g + 1 < NG)
            def _():
                start(c_dn(l, g + 1))

            @pl.when(g >= 2)
            def _():
                s0(i, g - 2)
            pbuf[g] = jnp.dot(ou[...], wdn[lax.rem(g, 2)], preferred_element_type=F32).astype(BF)
            k_d2d(i, g).start()
        s0(i, 2)

    a0(NC - 2)
    for name, g in TAIL_EV:
        handlers[name](NC - 1, g)
    a0(NC - 1)
    wait(c_kv(NC - 1))


def build(cfg, lens, x, cos, sin, wq, wk, wv, wo, wg, wu, wd, ng, qg, kg):
    CH, D, F, NH, HS = cfg["CH"], cfg["D"], cfg["F"], cfg["NH"], cfg["HS"]
    L, S = wq.shape[0], x.shape[1]
    OW = NH * HEAD
    GC = D // NG
    FT = cfg["FT"]
    any_ = pl.BlockSpec(memory_space=pltpu.HBM)
    vm = pl.BlockSpec(memory_space=pltpu.VMEM)
    V = pltpu.VMEM
    dma = pltpu.SemaphoreType.DMA
    T = 2 * S
    fl = L * (2 * T * D * (OW + 2 * HEAD + 2 * F) + 2 * T * (OW + F) * D)
    return pl.pallas_call(
        functools.partial(mega, cfg),
        name="mega",
        out_shape=(jax.ShapeDtypeStruct((L, 2, S, D), BF), jax.ShapeDtypeStruct((L, 2, S, HEAD), BF), jax.ShapeDtypeStruct((L, 2, S, HEAD), BF)),
        in_specs=[pl.BlockSpec(memory_space=pltpu.SMEM)] + [any_] * 10 + [vm] * 3,
        out_specs=(any_, any_, any_),
        scratch_shapes=[
            V((D, OW + 2 * HEAD), BF), V((2, D, 2 * FT), BF), V((2, OW + F, GC), BF),
            V((CH, D), BF), V((2, CH // 4, D), BF), V((CH, OW + F), BF),
            V((NG, CH, GC), BF), V((2, NG, CH // 2, GC), BF), V((2, NG, CH // 4, GC), BF), V((2, NG, CH // 8, GC), BF),
            V((CH // 8, D), BF), V((CH, OW + 2 * HEAD), F32), V((NH, CH, HEAD), BF), V((S, HEAD), BF), V((S, HEAD), BF),
            V((2, CH, HEAD), F32),
            dma((KINDS, 2, NG)), dma((KINDS, 2, NG)), dma((6, 3)), dma((4, NG)), dma((2,)),
        ],
        compiler_params=pltpu.CompilerParams(collective_id=0, has_side_effects=True, vmem_limit_bytes=66 * 10 ** 6),
        cost_estimate=pl.CostEstimate(flops=fl, bytes_accessed=200 * 2 ** 20, transcendentals=0),
    )(lens, x, cos, sin, wq, wk, wv, wo, wg, wu, wd, ng, qg, kg)


def rope_tables(positions):
    pair = jnp.arange(HEAD // 2, dtype=F32) * (2.0 / HEAD)
    freq = jnp.repeat(ROPE_THETA ** (-pair), 2)
    ang = positions.astype(F32)[:, :, None] * freq
    sign = jnp.where(jnp.arange(HEAD) % 2 == 0, -1.0, 1.0).astype(F32)
    return jnp.cos(ang), jnp.sin(ang) * sign


def solution(mesh, ch=512, ft=256):
    act = P("dp", None, None)
    col = P(None, None, "tp")
    row = P(None, "tp", None)
    cache = P(None, "dp", None, "tp", None)

    def body(x, positions, lengths, w_q, w_k, w_v, w_o, w_gate, w_up, w_down, norm_gain, q_gain, k_gain):
        L, S = w_q.shape[0], x.shape[1]
        hs = S // ch
        cfg = dict(CH=ch, D=x.shape[2], F=w_gate.shape[2], NH=q_gain.shape[1], NC=L * 2 * hs, HS=hs, FT=ft)
        cos, sin = rope_tables(positions)
        hy, kc, vc = build(cfg, lengths, x, cos, sin, w_q, w_k, w_v, w_o, w_gate, w_up, w_down, norm_gain, q_gain, k_gain)
        return hy[L - 1], kc[:, :, :, None, :], vc[:, :, :, None, :]

    return jax.shard_map(body, mesh=mesh, in_specs=(act, P("dp", None), P("dp"), col, col, col, row, col, col, row, P(None, None), row, row),
                         out_specs=(act, cache, cache), check_vma=False)
```

time: 1000 us -> 511 us (0.51)
  Pallas kernels: 0 us -> 487 us
  waiting for transfers between devices: 426 us -> 0 us
  matrix products: 411 us -> 0 us
  other arithmetic: 110 us -> 6.25 us
  local copies, waits for them, and re-layouts: 34.4 us -> 16.4 us
  between operations: 15 us -> 0.67 us
    pallas_call x0 -> x1, Pallas kernels: none -> 487 us  [build(): pl.pallas_call(functools.partial(mega, cfg), name='mega', out_shape=(jax....]
    psum x2 -> x0, waiting for transfers between devices: 425 us -> none  [device_body(): full_sum = lax.psum(part_sum.astype(jnp.bfloat16), 'tp')]
    dot_general x18 -> x0, matrix products: 411 us -> none  [the longest x2 82.6 us: branches(): jnp.dot(mlp_act, w_down, preferred_element_type=jnp.float32)]
    reduce_sum x10 -> x0, other arithmetic: 66.9 us -> none  [the longest x2 28.8 us: one_block(): attn_probs = jax.nn.softmax(scores, axis=-1).astype(jnp.bfloat16)]
    convert_element_type x4 -> x1, other arithmetic: 19.4 us -> 0.7 us  [rope_tables(): ang = positions.astype(F32)[:, :, None] * freq]
    dot_general x3 -> x0, local copies, waits for them, and re-layouts: 16.4 us -> none  [project(): jnp.dot(normed, w_q, preferred_element_type=jnp.float32)]
    squeeze x0 -> x1, local copies, waits for them, and re-layouts: none -> 14.2 us  [body(): return (hy[L - 1], kc[:, :, :, None, :], vc[:, :, :, None, :])]
  transfers between devices with their start and end apart: 2 -> 0, of which waited for: 2 -> 0; matrix products, arithmetic and copies ran while one was open for 1% -> 0% of each run, Pallas kernels for 0% -> 0%
where the time goes in v1:
time: 511 us; the launch traced here: 510 us
  Pallas kernels  487 us (95%)
  local copies, waits for them, and re-layouts  16.4 us (3%)
  other arithmetic  6.25 us (1%)
    pallas_call x1, Pallas kernels, build(): pl.pallas_call(functools.partial(mega, cfg), name='mega', out_shape=(jax....  487 us
    squeeze x1, local copies, waits for them, and re-layouts, body(): return (hy[L - 1], kc[:, :, :, None, :], vc[:, :, :, None, :])  14.2 us

profile of v1, /device:TPU:0, one launch (start us, length us, event | category | flops | bytes accessed | tf_op | source)
XLA Modules:
  0.0 510.4 jit_solution(432259363367984899)
XLA Ops:
  0.7 0.7 convert_element_type.3
  1.4 0.1 broadcast_in_dim.19
  1.4 0.1 mul.32
  1.6 5.5 %fusion = (f32[2,1024,128]{2,1,0:T(8,128)}, f32[2,1024,128]{2,1,0:T(8,128)}) fusion(f32[128]{0:T(128)S(1)} %compare_select_fusion, f32[128]{0:T(128)S(1)} %mul.32, f32[2,1024]{1,0:T(2,128)S(1)} %convert_element_type.3), kind=kLoop, calls=%fused_computation.3 | loop fusion | flops 524288 | bytes 2106368 | tf_op jit(solution)/shard_map/mul | solution.py:411
  7.1 487.2 %mega.1 = (bf16[2,2,1024,4096]{3,2,1,0:T(8,128)(2,1)}, bf16[2,2,1024,128]{3,2,1,0:T(8,128)(2,1)}, bf16[2,2,1024,128]{3,2,1,0:T(8,128)(2,1)}) custom-call(s32[2]{0:T(128)} %lens.1, bf16[2,1024,4096]{2,1,0:T(8,128)(2,1)} %x.1, f32[2,1024,128]{2,1,0:T(8,128)} %get-tuple-element.16.cos, f32[2,1024,128]{2,1,0:T(8,128)} %get-tuple-element.15.sin, ...), custom_call_target="tpu_custom_call" | custom-call | flops 223338299392 | bytes 209715200 | tf_op jit(solution)/shard_map/mega/pallas_call | solution.py:387
  494.3 0.0 copy-start.1
  494.3 0.0 copy-start
  494.3 14.2 %slice_bitcast_fusion = bf16[2,1024,4096]{2,1,0:T(8,128)(2,1)} fusion(bf16[2,2,1024,4096]{3,2,1,0:T(8,128)(2,1)} %get-tuple-element.6), kind=kLoop, calls=%fused_computation | loop fusion | bytes 33554432 | tf_op jit(solution)/shard_map/squeeze | solution.py:426
  508.5 0.0 copy-done.1
  508.5 1.0 copy.22
  509.5 0.0 copy-done
  509.5 1.0 copy.23
  (2 shorter events, 0.0 us)
Async XLA Ops:
  494.3 14.2 %copy-start.1 = (bf16[2,2,1024,128]{3,2,1,0:T(8,128)(2,1)S(1)}, bf16[2,2,1024,128]{3,2,1,0:T(8,128)(2,1)}, u32[]{:S(2)}) copy-start(bf16[2,2,1024,128]{3,2,1,0:T(8,128)(2,1)} %get-tuple-element.7) | copy-start | bytes 3145732
  494.3 15.2 %copy-start = (bf16[2,2,1024,128]{3,2,1,0:T(8,128)(2,1)S(1)}, bf16[2,2,1024,128]{3,2,1,0:T(8,128)(2,1)}, u32[]{:S(2)}) copy-start(bf16[2,2,1024,128]{3,2,1,0:T(8,128)(2,1)} %get-tuple-element.8) | copy-start | bytes 3145732

commit v2 on v1

v2 whole, which is shorter than its diff:
```python
import functools
import math

import jax
import jax.numpy as jnp
from jax import lax
from jax.experimental import pallas as pl
from jax.experimental.pallas import tpu as pltpu
from jax.sharding import PartitionSpec as P

HEAD = 128
ROPE_THETA = 75000000.0
NORM_EPS = 1e-5
BF = jnp.bfloat16
F32 = jnp.float32
MESH = pl.DeviceIdType.MESH
NG = 4
KINDS = 9
D2D, S1, S2, A2, A1A, A1B, A0A, A0B, A0C = range(KINDS)

Q_EV = [("a1", 2, 2)]
ROPE_EV = {0: [("s0", 1, 3), ("s1", 1, 0), ("a1", 2, 3)], 1: [("s1", 1, 1)]}
ATT_EV = [("s1", 1, 2)]
GU_EV = {2: [("s1", 1, 3), ("s2", 1, 0)], 3: [("s2", 1, 1)], 4: [("s2", 1, 2), ("a2", 1, 0), ("a0", 2, 0)], 5: [("s2", 1, 3)], 6: [("a2", 1, 1)]}
DN_EV = {0: [("a2", 1, 2)], 1: [("a2", 1, 3), ("a1", 1, 0)], 2: [("s0", 0, 0)], 3: [("s0", 0, 1), ("a1", 1, 1)]}
END_EV = [("s0", 0, 2)]
TAIL_EV = [("a1", 2, 2), ("a1", 2, 3), ("s0", 1, 3), ("s1", 1, 0), ("s1", 1, 1), ("s2", 1, 0), ("s1", 1, 2), ("s2", 1, 1), ("a2", 1, 0), ("s1", 1, 3), ("s2", 1, 2), ("a2", 1, 1), ("a1", 1, 0),
           ("s2", 1, 3), ("a2", 1, 2), ("a1", 1, 1), ("a2", 1, 3), ("a1", 1, 2), ("a1", 1, 3)]


def mo(v, m):
    return pl.multiple_of(v, m)


def mega(cfg, lens, x, cos, sin, wq, wk, wv, wo, wg, wu, wd, ng, qg, kg,
         hy, kc, vc,
         wqkv, ring, wdn, nbuf, hblk, ou, pbuf, d2d, s1b, s2b, res, qbuf, sbuf, prob, lbias, kbuf, vbuf, csb,
         ssem, rsem, wsem, lsem, osem):
    CH, D, F, NH, NC, HS = cfg["CH"], cfg["D"], cfg["F"], cfg["NH"], cfg["NC"], cfg["HS"]
    GC = D // NG
    FT = cfg["FT"]
    NT = F // FT
    OW = NH * HEAD
    S = HS * CH
    QB = CH // 4
    tp = lax.axis_index("tp")
    core = lax.rem(tp, 2)
    bx = lax.rem(lax.div(tp, 2), 2)
    by = lax.div(tp, 4)
    xn = tp + 2 - 4 * bx
    yn = tp + 4 - 8 * by
    cn = tp + 1 - 2 * core
    n1 = jnp.where(core == 0, xn, yn)
    n2 = jnp.where(core == 0, yn, xn)
    b1 = jnp.where(core == 0, bx, by)
    b2 = jnp.where(core == 0, by, bx)
    H2, H4, H8 = CH // 2, CH // 4, CH // 8
    my_row = core * H2 + b1 * H4 + b2 * H8

    def where(c):
        l = lax.div(c, 2 * HS)
        b = lax.rem(lax.div(c, HS), 2)
        s = lax.rem(c, HS)
        return l, b, s

    def rcopy(kind, c, g, src, dst, dev):
        par = lax.rem(c, 2)
        return pltpu.make_async_remote_copy(
            src_ref=src, dst_ref=dst, send_sem=ssem.at[kind, par, g], recv_sem=rsem.at[kind, par, g],
            device_id={"tp": dev}, device_id_type=MESH)

    def hrows(c, off, n, g):
        l, b, s = where(c)
        return hy.at[l, b, pl.ds(mo(s * CH + off, H8), n), pl.ds(mo(g * GC, GC), GC)]

    def k_d2d(c, g):
        par = lax.rem(c, 2)
        return rcopy(D2D, c, g, pbuf.at[g, pl.ds(mo((1 - core) * H2, H2), H2)], d2d.at[par, g], cn)

    def k_s1(c, g):
        par = lax.rem(c, 2)
        return rcopy(S1, c, g, d2d.at[par, g, pl.ds(mo((1 - b1) * H4, H4), H4)], s1b.at[par, g], n1)

    def k_s2(c, g):
        par = lax.rem(c, 2)
        return rcopy(S2, c, g, s1b.at[par, g, pl.ds(mo((1 - b2) * H8, H8), H8)], s2b.at[par, g], n2)

    def k_own(kind, c, g, dev):
        return rcopy(kind, c, g, s2b.at[lax.rem(c, 2), g], hrows(c, my_row, H8, g), dev)

    def k_fwd(kind, c, g, dev):
        if kind == A0C:
            off, n = core * H2 + (1 - b1) * H4, H4
        else:
            off, n = core * H2 + b1 * H4 + (1 - b2) * H8, H8
        ref = hrows(c, off, n, g)
        return rcopy(kind, c, g, ref, ref, dev)

    def k_loc(c, g):
        return pltpu.make_async_copy(s2b.at[lax.rem(c, 2), g], hrows(c, my_row, H8, g), lsem.at[2 + lax.rem(c, 2), g])

    def c_res(c):
        l, b, s = where(c)
        rows = pl.ds(mo(s * CH + my_row, H8), H8)
        return (pltpu.make_async_copy(x.at[b, rows], res, lsem.at[1, 0]),
                pltpu.make_async_copy(hy.at[0, b, rows], res, lsem.at[1, 0]))

    RB = min(32, H8)

    def s0(c, g):
        par = lax.rem(c, 2)
        cp = k_d2d(c, g)
        cp.wait_recv()
        cp.wait_send()

        @pl.loop(0, H2 // RB)
        def _(r):
            rr = pl.ds(mo(r * RB, RB), RB)
            d2d[par, g, rr] = d2d[par, g, rr] + pbuf[g, pl.ds(mo(core * H2 + r * RB, RB), RB)]
        k_s1(c, g).start()

    def s1(c, g):
        par = lax.rem(c, 2)
        cp = k_s1(c, g)
        cp.wait_recv()
        cp.wait_send()

        @pl.loop(0, H4 // RB)
        def _(r):
            rr = pl.ds(mo(r * RB, RB), RB)
            s1b[par, g, rr] = s1b[par, g, rr] + d2d[par, g, pl.ds(mo(b1 * H4 + r * RB, RB), RB)]
        k_s2(c, g).start()

    def s2(c, g):
        par = lax.rem(c, 2)
        cp = k_s2(c, g)
        cp.wait_recv()
        cp.wait_send()
        if g == 0:
            c_res(c)[0].wait()

        @pl.loop(0, H8 // RB)
        def _(r):
            rr = pl.ds(mo(r * RB, RB), RB)
            t = s2b[par, g, rr].astype(F32) + s1b[par, g, pl.ds(mo(b2 * H8 + r * RB, RB), RB)].astype(F32)
            s2b[par, g, rr] = (t + res[rr, pl.ds(g * GC, GC)].astype(F32)).astype(BF)
        k_own(A2, c, g, n2).start()
        k_own(A1A, c, g, n1).start()
        k_own(A0A, c, g, cn).start()
        k_loc(c, g).start()

    def a2(c, g):
        cp = k_own(A2, c, g, n2)
        cp.wait_recv()
        cp.wait_send()
        k_fwd(A1B, c, g, n1).start()
        k_fwd(A0B, c, g, cn).start()

    def a1(c, g):
        for cp in (k_own(A1A, c, g, n1), k_fwd(A1B, c, g, n1)):
            cp.wait_recv()
            cp.wait_send()
        k_fwd(A0C, c, g, cn).start()

    def a0(c, _):
        for g in range(NG):
            for cp in (k_own(A0A, c, g, cn), k_fwd(A0B, c, g, cn), k_fwd(A0C, c, g, cn)):
                cp.wait_recv()
                cp.wait_send()
            k_loc(c, g).wait()

    handlers = {"s0": s0, "s1": s1, "s2": s2, "a2": a2, "a1": a1, "a0": a0}

    def events(i, evs, extra=None):
        for lag in (2, 1, 0):
            now = [(name, g) for name, d, g in evs if d == lag]
            if not now:
                continue
            ok = i >= lag

            @pl.when(ok if extra is None else ok & extra)
            def _():
                for name, g in now:
                    handlers[name](i - lag, g)

    def c_qkv(l):
        return (pltpu.make_async_copy(wq.at[l], wqkv.at[:, pl.ds(0, OW)], wsem.at[5, 0]),
                pltpu.make_async_copy(wk.at[l], wqkv.at[:, pl.ds(OW, HEAD)], wsem.at[5, 1]),
                pltpu.make_async_copy(wv.at[l], wqkv.at[:, pl.ds(OW + HEAD, HEAD)], wsem.at[5, 2]))

    def c_gu(c, j):
        l = where(c)[0]
        sl = lax.rem(c * NT + j, 3)
        cc = pl.ds(mo(j * FT, FT), FT)
        return (pltpu.make_async_copy(wg.at[l, :, cc], ring.at[sl, :, pl.ds(0, FT)], wsem.at[0, sl]),
                pltpu.make_async_copy(wu.at[l, :, cc], ring.at[sl, :, pl.ds(FT, FT)], wsem.at[1, sl]))

    def c_dn(l, g):
        sl = lax.rem(g, 2)
        cc = pl.ds(mo(g * GC, GC), GC)
        return (pltpu.make_async_copy(wo.at[l, :, cc], wdn.at[sl, pl.ds(0, OW)], wsem.at[2, sl]),
                pltpu.make_async_copy(wd.at[l, :, cc], wdn.at[sl, pl.ds(OW, F)], wsem.at[3, sl]))

    UB, UN = CH // 8, 5
    US = (CH - UN * UB) // NG

    def c_h(c, off, n, sl):
        l, b, s = where(c)
        rows = pl.ds(mo(s * CH + off, 16), n)
        dst = hblk.at[sl, pl.ds(0, n)]
        return (pltpu.make_async_copy(x.at[b, rows], dst, lsem.at[0, sl]),
                pltpu.make_async_copy(hy.at[0, b, rows], dst, lsem.at[0, sl]))

    def c_hgu(c, u):
        return c_h(c, u * UB, UB, lax.rem(u, 2))

    def c_hdn(c, g):
        return c_h(c, UN * UB + g * US, US, lax.rem(UN + g, 2))

    def c_cs(c):
        l, b, s = where(c)
        rows = pl.ds(mo(s * CH, CH), CH)
        return (pltpu.make_async_copy(cos.at[b, rows], csb.at[0], wsem.at[4, 0]),
                pltpu.make_async_copy(sin.at[b, rows], csb.at[1], wsem.at[4, 1]))

    def c_kv(c):
        l, b, s = where(c)
        rows = pl.ds(mo(s * CH, CH), CH)
        return (pltpu.make_async_copy(kbuf.at[rows], kc.at[l, b, rows], osem.at[0]),
                pltpu.make_async_copy(vbuf.at[rows], vc.at[l, b, rows], osem.at[1]))

    def start(cps):
        for cp in cps:
            cp.start(priority=1)

    def wait(cps):
        for cp in cps:
            cp.wait()

    def start_by_layer(c, pair):
        @pl.when(c < 2 * HS)
        def _():
            pair[0].start()

        @pl.when(c >= 2 * HS)
        def _():
            pair[1].start()

    bar = pltpu.get_barrier_semaphore()
    for dev in (xn, yn, cn):
        pl.semaphore_signal(bar, inc=1, device_id={"tp": dev}, device_id_type=MESH)

    def ln_rows(src, dst, gain, n):
        for q in range(n // 16):
            v = src(q).astype(F32)
            mean = jnp.sum(v, axis=1, keepdims=True) * (1.0 / D)
            v = v - mean
            var = jnp.sum(v * v, axis=1, keepdims=True) * (1.0 / D)
            dst(q, (v * lax.rsqrt(var + NORM_EPS) * gain).astype(BF))

    def ln_first(src, dst, gain, n):
        means = [jnp.sum(src(q).astype(F32), axis=1, keepdims=True) * (1.0 / D) for q in range(n // 16)]
        rs = []
        for q in range(n // 16):
            v = src(q).astype(F32) - means[q]
            rs.append(lax.rsqrt(jnp.sum(v * v, axis=1, keepdims=True) * (1.0 / D) + NORM_EPS))
        for q in range(n // 16):
            dst(q, ((src(q).astype(F32) - means[q]) * rs[q] * gain).astype(BF))

    def ln_next(i, off, n, sl):
        par = lax.rem(i + 1, 2)
        gain = ng[pl.ds(jnp.minimum(lax.div(i + 1, 2 * HS), ng.shape[0] - 1), 1), :]

        def put(q, v):
            nbuf[par, pl.ds(mo(off + q * 16, 16), 16), :] = v
        ln_rows(lambda q: hblk[sl, pl.ds(q * 16, 16), :], put, gain, n)

    def first(k):
        rows = pl.ds(mo(k * UB, UB), UB)
        return pltpu.make_async_copy(x.at[0, rows], nbuf.at[1, rows], lsem.at[2 + lax.div(k, 4), lax.rem(k, 4)])

    for k in range(8):
        first(k).start()
    start(c_qkv(0))
    for cp in c_cs(0):
        cp.start()
    start(c_gu(0, 0))
    start(c_gu(0, 1))
    gain0 = ng[pl.ds(0, 1), :]

    @pl.loop(0, 8)
    def _(k):
        first(k).wait()

        def put(q, v):
            nbuf[0, pl.ds(mo(k * UB + q * 16, 16), 16), :] = v
        ln_first(lambda q: nbuf[1, pl.ds(mo(k * UB + q * 16, 16), 16), :], put, gain0, UB)

    pl.semaphore_wait(bar, 3)
    lane = lax.broadcasted_iota(jnp.int32, (CH // 2, HEAD), 1)
    even = lax.rem(lane, 2) == 0

    @pl.loop(0, NC)
    def _(i):
        l, b, s = where(i)
        np_ = lax.rem(i, 2)
        more = i + 1 < NC
        lnext = where(i + 1)[0]

        wait(c_qkv(l))
        events(i, Q_EV)

        @pl.when(i > 0)
        def _():
            wait(c_kv(i - 1))
        wait(c_cs(i))
        sbuf[1, :, pl.ds(0, OW + 2 * HEAD)] = jnp.dot(nbuf[np_], wqkv[...], preferred_element_type=F32)

        def gu(j):
            r = jnp.dot(nbuf[np_], ring[lax.rem(i * NT + j, 3)], preferred_element_type=F32)
            ou[:, pl.ds(mo(OW + j * FT, 128), FT)] = (jax.nn.silu(r[:, :FT]) * r[:, FT:]).astype(BF)

        @pl.loop(0, 2)
        def _(j):
            wait(c_gu(i, j))
            start(c_gu(i, j + 2))
            for k, evs in ROPE_EV.items():
                events(i, evs, j == k)
            rr = pl.ds(mo(j * H2, H2), H2)
            ct = csb[0, rr]
            st = csb[1, rr]

            def norm_rope(v, gvec):
                mean = jnp.sum(v, axis=1, keepdims=True) * (1.0 / HEAD)
                v = v - mean
                var = jnp.sum(v * v, axis=1, keepdims=True) * (1.0 / HEAD)
                v = v * lax.rsqrt(var + NORM_EPS) * gvec
                sw = jnp.where(even, pltpu.roll(v, HEAD - 1, 1), pltpu.roll(v, 1, 1))
                return (v * ct + sw * st).astype(BF)
            for h in range(NH):
                qbuf[h, rr] = norm_rope(sbuf[1, rr, pl.ds(h * HEAD, HEAD)], qg[l, pl.ds(h, 1), :])
            ks = pl.ds(mo(s * CH + j * H2, H2), H2)
            kbuf[ks] = norm_rope(sbuf[1, rr, pl.ds(OW, HEAD)], kg[l])
            vbuf[ks] = sbuf[1, rr, pl.ds(OW + HEAD, HEAD)].astype(BF)
            gu(j)

        for cp in c_kv(i):
            cp.start()

        @pl.when(more)
        def _():
            for cp in c_cs(i + 1):
                cp.start()
            start_by_layer(i + 1, c_hgu(i + 1, 0))
        events(i, ATT_EV)
        rlen = lens[b]
        sscale = HEAD ** -0.5 * math.log2(math.e)

        def qk(ss, qb):
            q4 = qbuf[:, pl.ds(qb * QB, QB), :].reshape(NH * QB, HEAD)
            nk = ss * CH + (qb + 1) * QB
            sbuf[qb % 2, :, pl.ds(0, nk)] = lax.dot_general(q4, kbuf[pl.ds(0, nk)], (((1,), (1,)), ((), ())), preferred_element_type=F32)

        def pref(qb, rows, cols):
            return prob.at[rows, cols] if qb % 2 == 0 else ou.at[rows, pl.ds(OW + F - S + cols.start, cols.size)]

        def softmax(ss, qb):
            full = ss * CH + qb * QB
            nk = full + QB
            sl = qb % 2
            rid = lax.broadcasted_iota(jnp.int32, (16, QB), 0)
            cid = lax.broadcasted_iota(jnp.int32, (16, QB), 1)
            for r in range(QB // 16):
                tri = jnp.where(cid <= rid + r * 16, 0.0, -1e30)
                for h in range(NH):
                    rows = pl.ds(h * QB + r * 16, 16)
                    t = sbuf[sl, rows, pl.ds(0, nk)] * sscale + lbias[:, pl.ds(0, nk)]
                    d = t[:, full:] + tri
                    m = jnp.max(d, axis=1, keepdims=True)
                    if full:
                        t = t[:, :full]
                        m = jnp.maximum(m, jnp.max(t, axis=1, keepdims=True))
                        e = jnp.exp2(t - m)
                        ed = jnp.exp2(d - m)
                        inv = 1.0 / (jnp.sum(e, axis=1, keepdims=True) + jnp.sum(ed, axis=1, keepdims=True))
                        pref(qb, rows, pl.ds(0, full))[...] = (e * inv).astype(BF)
                    else:
                        ed = jnp.exp2(d - m)
                        inv = 1.0 / jnp.sum(ed, axis=1, keepdims=True)
                    pref(qb, rows, pl.ds(full, QB))[...] = (ed * inv).astype(BF)

        def pv(ss, qb):
            nk = ss * CH + (qb + 1) * QB
            o = jnp.dot(pref(qb, pl.ds(0, CH), pl.ds(0, nk))[...], vbuf[pl.ds(0, nk)], preferred_element_type=F32).astype(BF)
            for h in range(NH):
                ou[pl.ds(qb * QB, QB), pl.ds(h * HEAD, HEAD)] = o[h * QB:(h + 1) * QB]

        lbias[...] = jnp.where(lax.broadcasted_iota(jnp.int32, lbias.shape, 1) < rlen, 0.0, -1e30)

        for ss in range(HS):
            @pl.when(s == ss)
            def _():
                qk(ss, 0)
                for qb in range(4):
                    if qb < 3:
                        qk(ss, qb + 1)
                    softmax(ss, qb)
                    pv(ss, qb)

        @pl.loop(2, NT)
        def _(j):
            wait(c_gu(i, j))

            @pl.when(j + 2 < NT)
            def _():
                start(c_gu(i, j + 2))

            @pl.when(j + 2 == NT)
            def _():
                start(c_dn(l, 0))

            @pl.when(j + 1 == NT)
            def _():
                start(c_dn(l, 1))

            @pl.when((j == 2) & more)
            def _():
                start(c_qkv(lnext))

            @pl.when(more)
            def _():
                c_hgu(i + 1, j - 2)[0].wait()

                @pl.when(j + 1 < NT)
                def _():
                    start_by_layer(i + 1, c_hgu(i + 1, j - 1))

                @pl.when(j + 1 == NT)
                def _():
                    start_by_layer(i + 1, c_hdn(i + 1, 0))
            for k, evs in GU_EV.items():
                events(i, evs, j == k)
            gu(j)
            ln_next(i, (j - 2) * UB, UB, lax.rem(j, 2))

        start_by_layer(i, c_res(i))

        @pl.loop(0, NG)
        def _(g):
            wait(c_dn(l, g))

            @pl.when((g >= 1) & (g + 1 < NG))
            def _():
                start(c_dn(l, g + 1))

            @pl.when((g >= 2) & more)
            def _():
                start(c_gu(i + 1, g - 2))

            @pl.when(more)
            def _():
                c_hdn(i + 1, g)[0].wait()

                @pl.when(g + 1 < NG)
                def _():
                    start_by_layer(i + 1, c_hdn(i + 1, g + 1))
            for k, evs in DN_EV.items():
                events(i, evs, g == k)
            pbuf[g] = jnp.dot(ou[...], wdn[lax.rem(g, 2)], preferred_element_type=F32).astype(BF)
            ln_next(i, UN * UB + g * US, US, lax.rem(UN + g, 2))
            k_d2d(i, g).start()
        events(i, END_EV)

    for name, lag, g in TAIL_EV:
        handlers[name](NC - lag, g)
    a0(NC - 2, 0)
    a0(NC - 1, 0)
    wait(c_kv(NC - 1))


def build(cfg, lens, x, cos, sin, wq, wk, wv, wo, wg, wu, wd, ng, qg, kg):
    CH, D, F, NH, HS = cfg["CH"], cfg["D"], cfg["F"], cfg["NH"], cfg["HS"]
    L, S = wq.shape[0], x.shape[1]
    OW = NH * HEAD
    GC = D // NG
    FT = cfg["FT"]
    any_ = pl.BlockSpec(memory_space=pltpu.HBM)
    vm = pl.BlockSpec(memory_space=pltpu.VMEM)
    V = pltpu.VMEM
    dma = pltpu.SemaphoreType.DMA
    T = 2 * S
    fl = L * (2 * T * D * (OW + 2 * HEAD + 2 * F) + 2 * T * (OW + F) * D)
    return pl.pallas_call(
        functools.partial(mega, cfg),
        name="mega",
        out_shape=(jax.ShapeDtypeStruct((L, 2, S, D), BF), jax.ShapeDtypeStruct((L, 2, S, HEAD), BF), jax.ShapeDtypeStruct((L, 2, S, HEAD), BF)),
        in_specs=[pl.BlockSpec(memory_space=pltpu.SMEM)] + [any_] * 10 + [vm] * 3,
        out_specs=(any_, any_, any_),
        scratch_shapes=[
            V((D, OW + 2 * HEAD), BF), V((3, D, 2 * FT), BF), V((2, OW + F, GC), BF),
            V((2, CH, D), BF), V((2, CH // 8, D), BF), V((CH, OW + F), BF),
            V((NG, CH, GC), BF), V((2, NG, CH // 2, GC), BF), V((2, NG, CH // 4, GC), BF), V((2, NG, CH // 8, GC), BF),
            V((CH // 8, D), BF), V((NH, CH, HEAD), BF), V((2, NH * CH // 4, S), F32), V((NH * CH // 4, S), BF), V((16, S), F32), V((S, HEAD), BF), V((S, HEAD), BF),
            V((2, CH, HEAD), F32),
            dma((KINDS, 2, NG)), dma((KINDS, 2, NG)), dma((6, 3)), dma((4, NG)), dma((2,)),
        ],
        compiler_params=pltpu.CompilerParams(collective_id=0, has_side_effects=True, vmem_limit_bytes=67 * 10 ** 6),
        cost_estimate=pl.CostEstimate(flops=fl, bytes_accessed=200 * 2 ** 20, transcendentals=0),
    )(lens, x, cos, sin, wq, wk, wv, wo, wg, wu, wd, ng, qg, kg)


def copy_out(hy, kc, vc, y, ko, vo, buf, kbuf, vbuf, sem, ksem):
    L = hy.shape[0]
    n = buf.shape[0]
    per = n // 2
    rows = hy.shape[2] // per
    cin, cout = [], []
    for k in range(n):
        at = (k // per, pl.ds(k % per * rows, rows))
        cin.append(pltpu.make_async_copy(hy.at[(L - 1,) + at], buf.at[k], sem.at[0, k]))
        cout.append(pltpu.make_async_copy(buf.at[k], y.at[at], sem.at[1, k]))
    for q, (src, tmp, dst) in enumerate(((kc, kbuf, ko), (vc, vbuf, vo))):
        cin.append(pltpu.make_async_copy(src, tmp, ksem.at[0, q]))
        cout.append(pltpu.make_async_copy(tmp, dst, ksem.at[1, q]))
    for cp in cin:
        cp.start()
    for a, b in zip(cin, cout):
        a.wait()
        b.start()
    for cp in cout:
        cp.wait()


def detach(hy, kc, vc):
    any_ = pl.BlockSpec(memory_space=pltpu.HBM)
    _, B, S, D = hy.shape
    n = 16
    return pl.pallas_call(
        copy_out, name="copy_out",
        out_shape=(jax.ShapeDtypeStruct((B, S, D), BF), jax.ShapeDtypeStruct(kc.shape, BF), jax.ShapeDtypeStruct(vc.shape, BF)),
        in_specs=[any_] * 3, out_specs=(any_,) * 3,
        scratch_shapes=[pltpu.VMEM((n, B * S // n, D), BF), pltpu.VMEM(kc.shape, BF), pltpu.VMEM(vc.shape, BF),
                        pltpu.SemaphoreType.DMA((2, n)), pltpu.SemaphoreType.DMA((2, 2))],
        compiler_params=pltpu.CompilerParams(vmem_limit_bytes=48 * 2 ** 20),
    )(hy, kc, vc)


def rope_tables(positions):
    pair = jnp.arange(HEAD // 2, dtype=F32) * (2.0 / HEAD)
    freq = jnp.repeat(ROPE_THETA ** (-pair), 2)
    ang = positions.astype(F32)[:, :, None] * freq
    sign = jnp.where(jnp.arange(HEAD) % 2 == 0, -1.0, 1.0).astype(F32)
    return jnp.cos(ang), jnp.sin(ang) * sign


def solution(mesh, ch=512, ft=256):
    act = P("dp", None, None)
    col = P(None, None, "tp")
    row = P(None, "tp", None)
    cache = P(None, "dp", None, "tp", None)

    def body(x, positions, lengths, w_q, w_k, w_v, w_o, w_gate, w_up, w_down, norm_gain, q_gain, k_gain):
        L, S = w_q.shape[0], x.shape[1]
        hs = S // ch
        cfg = dict(CH=ch, D=x.shape[2], F=w_gate.shape[2], NH=q_gain.shape[1], NC=L * 2 * hs, HS=hs, FT=ft)
        cos, sin = rope_tables(positions)
        hy, kc, vc = build(cfg, lengths, x, cos, sin, w_q, w_k, w_v, w_o, w_gate, w_up, w_down, norm_gain, q_gain, k_gain)
        y, kc, vc = detach(hy, kc, vc)
        return y, kc[:, :, :, None, :], vc[:, :, :, None, :]

    return jax.shard_map(body, mesh=mesh, in_specs=(act, P("dp", None), P("dp"), col, col, col, row, col, col, row, P(None, None), row, row),
                         out_specs=(act, cache, cache), check_vma=False)
```

time: 511 us -> 366 us (0.72)
  Pallas kernels: 487 us -> 356 us
  local copies, waits for them, and re-layouts: 16.4 us -> 2.65 us
    pallas_call x1, Pallas kernels: 487 us -> 343 us  [build(): pl.pallas_call(functools.partial(mega, cfg), name='mega', out_shape=(jax....]
    squeeze x1 -> x0, local copies, waits for them, and re-layouts: 14.2 us -> none  [body(): return (hy[L - 1], kc[:, :, :, None, :], vc[:, :, :, None, :])]
    pallas_call x0 -> x1, Pallas kernels: none -> 12.7 us  [detach(): pl.pallas_call(copy_out, name='copy_out', out_shape=(jax.ShapeDtypeStruct...]
where the time goes in v2:
time: 366 us; the launch traced here: 365 us
  Pallas kernels  356 us (97%)
  other arithmetic  6.25 us (2%)
    pallas_call x1, Pallas kernels, build(): pl.pallas_call(functools.partial(mega, cfg), name='mega', out_shape=(jax....  343 us
    pallas_call x1, Pallas kernels, detach(): pl.pallas_call(copy_out, name='copy_out', out_shape=(jax.ShapeDtypeStruct...  12.7 us

profile of v2, /device:TPU:0, one launch (start us, length us, event | category | flops | bytes accessed | tf_op | source)
XLA Modules:
  0.0 365.5 jit_solution(5129087425854891322)
XLA Ops:
  0.7 0.7 convert_element_type.3
  1.4 0.1 broadcast_in_dim.19
  1.4 0.1 mul.32
  1.6 5.5 %fusion = (f32[2,1024,128]{2,1,0:T(8,128)}, f32[2,1024,128]{2,1,0:T(8,128)}) fusion(f32[128]{0:T(128)S(1)} %compare_select_fusion, f32[128]{0:T(128)S(1)} %mul.32, f32[2,1024]{1,0:T(2,128)S(1)} %convert_element_type.3), kind=kLoop, calls=%fused_computation.2 | loop fusion | flops 524288 | bytes 2106368 | tf_op jit(solution)/shard_map/mul | solution.py:553
  7.1 343.2 %mega.1 = (bf16[2,2,1024,4096]{3,2,1,0:T(8,128)(2,1)}, bf16[2,2,1024,128]{3,2,1,0:T(8,128)(2,1)}, bf16[2,2,1024,128]{3,2,1,0:T(8,128)(2,1)}) custom-call(s32[2]{0:T(128)} %lens.1, bf16[2,1024,4096]{2,1,0:T(8,128)(2,1)} %x.1, f32[2,1024,128]{2,1,0:T(8,128)} %get-tuple-element.22.cos, f32[2,1024,128]{2,1,0:T(8,128)} %get-tuple-element.21.sin, ...), custom_call_target="tpu_custom_call" | custom-call | flops 223338299392 | bytes 209715200 | tf_op jit(solution)/shard_map/mega/pallas_call | solution.py:493
  350.3 0.0 copy-start
  350.3 1.2 copy-done
  351.5 0.0 copy-start.1
  351.5 1.2 copy-done.1
  352.8 12.7 %copy_out.1 = (bf16[2,1024,4096]{2,1,0:T(8,128)(2,1)}, bf16[2,2,1024,128]{3,2,1,0:T(8,128)(2,1)}, bf16[2,2,1024,128]{3,2,1,0:T(8,128)(2,1)}) custom-call(bf16[2,2,1024,4096]{3,2,1,0:T(8,128)(2,1)} %get-tuple-element.9.hy, bf16[2,2,1024,128]{3,2,1,0:T(8,128)(2,1)S(1)} %copy-done, bf16[2,2,1024,128]{3,2,1,0:T(8,128)(2,1)S(1)} %copy-done.1), custom_call_target="tpu_custom_call" | custom-call | tf_op jit(solution)/shard_map/copy_out/pallas_call | solution.py:538
  (2 shorter events, 0.0 us)
Async XLA Ops:
  350.3 1.2 copy-start
  351.5 1.2 copy-start.1

commit v3 on v2

--- a/solution.py
+++ b/solution.py
@@ -21,7 +21,7 @@
 Q_EV = [("a1", 2, 2)]
 ROPE_EV = {0: [("s0", 1, 3), ("s1", 1, 0), ("a1", 2, 3)], 1: [("s1", 1, 1)]}
 ATT_EV = [("s1", 1, 2)]
-GU_EV = {2: [("s1", 1, 3), ("s2", 1, 0)], 3: [("s2", 1, 1)], 4: [("s2", 1, 2), ("a2", 1, 0), ("a0", 2, 0)], 5: [("s2", 1, 3)], 6: [("a2", 1, 1)]}
+GU_EV = {2: [("s2", 1, 0)], 3: [("s1", 1, 3), ("s2", 1, 1)], 4: [("s2", 1, 2), ("a0", 2, 0)], 5: [("s2", 1, 3), ("a2", 1, 0)], 6: [("a2", 1, 1)]}
 DN_EV = {0: [("a2", 1, 2)], 1: [("a2", 1, 3), ("a1", 1, 0)], 2: [("s0", 0, 0)], 3: [("s0", 0, 1), ("a1", 1, 1)]}
 END_EV = [("s0", 0, 2)]
 TAIL_EV = [("a1", 2, 2), ("a1", 2, 3), ("s0", 1, 3), ("s1", 1, 0), ("s1", 1, 1), ("s2", 1, 0), ("s1", 1, 2), ("s2", 1, 1), ("a2", 1, 0), ("s1", 1, 3), ("s2", 1, 2), ("a2", 1, 1), ("a1", 1, 0),

time: 366 us -> 349 us (0.954)
  Pallas kernels: 356 us -> 340 us
    pallas_call x1, Pallas kernels: 343 us -> 327 us  [build(): pl.pallas_call(functools.partial(mega, cfg), name='mega', out_shape=(jax....]
where the time goes in v3:
time: 349 us
  Pallas kernels  340 us (97%)
  other arithmetic  6.25 us (2%)
    pallas_call x1, Pallas kernels, build(): pl.pallas_call(functools.partial(mega, cfg), name='mega', out_shape=(jax....  327 us
    pallas_call x1, Pallas kernels, detach(): pl.pallas_call(copy_out, name='copy_out', out_shape=(jax.ShapeDtypeStruct...  12.7 us

profile of v3, /device:TPU:0, one launch (start us, length us, event | category | flops | bytes accessed | tf_op | source)
XLA Modules:
  0.0 349.1 jit_solution(16953387230692898146)
XLA Ops:
  0.7 0.7 convert_element_type.3
  1.4 0.1 broadcast_in_dim.19
  1.4 0.1 mul.32
  1.6 5.5 %fusion = (f32[2,1024,128]{2,1,0:T(8,128)}, f32[2,1024,128]{2,1,0:T(8,128)}) fusion(f32[128]{0:T(128)S(1)} %compare_select_fusion, f32[128]{0:T(128)S(1)} %mul.32, f32[2,1024]{1,0:T(2,128)S(1)} %convert_element_type.3), kind=kLoop, calls=%fused_computation.2 | loop fusion | flops 524288 | bytes 2106368 | tf_op jit(solution)/shard_map/mul | solution.py:553
  7.1 326.9 %mega.1 = (bf16[2,2,1024,4096]{3,2,1,0:T(8,128)(2,1)}, bf16[2,2,1024,128]{3,2,1,0:T(8,128)(2,1)}, bf16[2,2,1024,128]{3,2,1,0:T(8,128)(2,1)}) custom-call(s32[2]{0:T(128)} %lens.1, bf16[2,1024,4096]{2,1,0:T(8,128)(2,1)} %x.1, f32[2,1024,128]{2,1,0:T(8,128)} %get-tuple-element.22.cos, f32[2,1024,128]{2,1,0:T(8,128)} %get-tuple-element.21.sin, ...), custom_call_target="tpu_custom_call" | custom-call | flops 223338299392 | bytes 209715200 | tf_op jit(solution)/shard_map/mega/pallas_call | solution.py:493
  334.0 0.0 copy-start
  334.0 1.2 copy-done
  335.2 0.0 copy-start.1
  335.2 1.2 copy-done.1
  336.4 12.7 %copy_out.1 = (bf16[2,1024,4096]{2,1,0:T(8,128)(2,1)}, bf16[2,2,1024,128]{3,2,1,0:T(8,128)(2,1)}, bf16[2,2,1024,128]{3,2,1,0:T(8,128)(2,1)}) custom-call(bf16[2,2,1024,4096]{3,2,1,0:T(8,128)(2,1)} %get-tuple-element.9.hy, bf16[2,2,1024,128]{3,2,1,0:T(8,128)(2,1)S(1)} %copy-done, bf16[2,2,1024,128]{3,2,1,0:T(8,128)(2,1)S(1)} %copy-done.1), custom_call_target="tpu_custom_call" | custom-call | tf_op jit(solution)/shard_map/copy_out/pallas_call | solution.py:538
  (2 shorter events, 0.0 us)
Async XLA Ops:
  334.0 1.2 copy-start
  335.2 1.2 copy-start.1
